TPU v7x, 32 devices: a whole 2x2x4 slice. The times are simulated.
32 devices in a mesh: dp: 4 (over x, y), tp: 8 (over z, core).
Axes of the slice: x: 2, y: 2, z: 4, core: 2. Of those that a mesh axis runs over, the one named last changes fastest.
Arguments:
- residual: bfloat16 [512, 3072], P('dp'), parts along dimension 0
- positions: int32 [512], P('dp'), parts along dimension 0
- ln1_gain: bfloat16 [3072], replicated
- ln1_shift: bfloat16 [3072], replicated
- w_q: bfloat16 [3072, 3072], P(None, 'tp')
- w_k: bfloat16 [3072, 1024], P(None, 'tp')
- w_v: bfloat16 [3072, 1024], P(None, 'tp')
- w_o: bfloat16 [3072, 3072], P('tp')
- ln2_gain: bfloat16 [3072], replicated
- ln2_shift: bfloat16 [3072], replicated
- w_up: bfloat16 [3072, 9216], P(None, 'tp')
- w_down: bfloat16 [9216, 3072], P('tp')
- k_cache: bfloat16 [512, 512, 8, 128], P('dp', None, 'tp'), parts along dimension 0
- v_cache: bfloat16 [512, 512, 8, 128], P('dp', None, 'tp'), parts along dimension 0
Outputs:
- output 1: bfloat16 [512, 3072], P('dp'), parts along dimension 0
- output 2: bfloat16 [512, 8, 128], P('dp', 'tp'), parts along dimension 0
- output 3: bfloat16 [512, 8, 128], P('dp', 'tp'), parts along dimension 0
There are 4 independent parts. A program takes and returns all parts, laid end to end along the dimension named above; an argument that names none is the same for every part.
All inputs are finite; a program needn't handle non-finite values.
Results may differ from a plain program's by a relative error of at most 0.0165008.
Values are sent between devices in bfloat16 or wider.
A program may use at most 1 GiB of HBM per device.

v0:
```python
import math
import jax
import jax.numpy as jnp
from jax import lax
from jax.sharding import PartitionSpec as P

LN_EPS = 1e-5
ROPE_BASE = 10000.0


def layer_norm_1p(row_block, gain_vec, shift_vec):
    block32 = row_block.astype(jnp.float32)
    row_mean = jnp.mean(block32, axis=-1, keepdims=True)
    centered = block32 - row_mean
    row_var = jnp.mean(centered * centered, axis=-1, keepdims=True)
    normed = centered * lax.rsqrt(row_var + LN_EPS)
    scaled = normed * (1.0 + gain_vec.astype(jnp.float32)) + shift_vec.astype(jnp.float32)
    return scaled.astype(jnp.bfloat16)


def rotate_first_half(head_vecs, positions):
    head_dim = head_vecs.shape[-1]
    rot_dim = head_dim // 2
    half_rot = rot_dim // 2
    inv_freq = jnp.power(ROPE_BASE, -2.0 * jnp.arange(half_rot, dtype=jnp.float32) / rot_dim)
    angles = positions.astype(jnp.float32)[:, None] * inv_freq[None, :]
    table_shape = (head_vecs.shape[0],) + (1,) * (head_vecs.ndim - 2) + (half_rot,)
    cos_table = jnp.cos(angles).reshape(table_shape)
    sin_table = jnp.sin(angles).reshape(table_shape)
    vecs32 = head_vecs.astype(jnp.float32)
    first_half = vecs32[..., :half_rot]
    second_half = vecs32[..., half_rot:rot_dim]
    turned = jnp.concatenate([first_half * cos_table - second_half * sin_table, second_half * cos_table + first_half * sin_table, vecs32[..., rot_dim:]], axis=-1)
    return turned.astype(jnp.bfloat16)


def attend(q_rot, k_rot, v_heads, k_cache, v_cache, positions):
    row_count = k_cache.shape[0]
    seq_max = k_cache.shape[1]
    score_scale = 1.0 / math.sqrt(k_cache.shape[3])
    old_scores = jnp.einsum('rkgd,rskd->rkgs', q_rot, k_cache, preferred_element_type=jnp.float32)
    new_scores = jnp.einsum('rkgd,rkd->rkg', q_rot, k_rot, preferred_element_type=jnp.float32)
    seq_index = jnp.arange(seq_max)[None, :]
    at_pos = (seq_index == positions[:, None])[:, None, None, :]
    valid_mask = (seq_index <= positions[:, None])[:, None, None, :]
    scores = jnp.where(at_pos, new_scores[..., None], old_scores) * score_scale
    scores = jnp.where(valid_mask, scores, -jnp.inf)
    prob_map = jax.nn.softmax(scores, axis=-1).astype(jnp.bfloat16)
    zero_bf = jnp.zeros((), jnp.bfloat16)
    old_probs = jnp.where(at_pos, zero_bf, prob_map)
    new_prob = jnp.sum(jnp.where(at_pos, prob_map, zero_bf).astype(jnp.float32), axis=-1)
    context = jnp.einsum('rkgs,rskd->rkgd', old_probs, v_cache, preferred_element_type=jnp.float32)
    context = context + new_prob[..., None] * v_heads.astype(jnp.float32)[:, :, None, :]
    return context.astype(jnp.bfloat16).reshape(row_count, -1)


def solution(mesh):
    row_spec = P('dp', None)
    whole_spec = P()
    col_spec = P(None, 'tp')
    wrow_spec = P('tp', None)
    cache_spec = P('dp', None, 'tp', None)
    new_spec = P('dp', 'tp', None)
    arg_specs = (row_spec, P('dp'), whole_spec, whole_spec, col_spec, col_spec, col_spec, wrow_spec, whole_spec, whole_spec, col_spec, wrow_spec, cache_spec, cache_spec)

    def local_step(residual, positions, ln1_gain, ln1_shift, w_q, w_k, w_v, w_o, ln2_gain, ln2_shift, w_up, w_down, k_cache, v_cache):
        row_count = residual.shape[0]
        slots_here = k_cache.shape[2]
        head_dim = k_cache.shape[3]
        group_size = w_q.shape[1] // (head_dim * slots_here)
        normed = layer_norm_1p(residual, ln1_gain, ln1_shift)
        q_proj = jnp.dot(normed, w_q, preferred_element_type=jnp.float32).astype(jnp.bfloat16)
        k_proj = jnp.dot(normed, w_k, preferred_element_type=jnp.float32).astype(jnp.bfloat16)
        v_proj = jnp.dot(normed, w_v, preferred_element_type=jnp.float32).astype(jnp.bfloat16)
        q_rot = rotate_first_half(q_proj.reshape(row_count, slots_here, group_size, head_dim), positions)
        k_rot = rotate_first_half(k_proj.reshape(row_count, slots_here, head_dim), positions)
        v_heads = v_proj.reshape(row_count, slots_here, head_dim)
        context = attend(q_rot, k_rot, v_heads, k_cache, v_cache, positions)
        attn_part = jnp.dot(context, w_o, preferred_element_type=jnp.float32).astype(jnp.bfloat16)
        attn_sum = lax.psum(attn_part, 'tp')
        after_attn = (residual.astype(jnp.float32) + attn_sum.astype(jnp.float32)).astype(jnp.bfloat16)
        normed_mid = layer_norm_1p(after_attn, ln2_gain, ln2_shift)
        up_proj = jnp.dot(normed_mid, w_up, preferred_element_type=jnp.float32)
        activated = jnp.square(jnp.maximum(up_proj, 0.0)).astype(jnp.bfloat16)
        mlp_part = jnp.dot(activated, w_down, preferred_element_type=jnp.float32).astype(jnp.bfloat16)
        mlp_sum = lax.psum(mlp_part, 'tp')
        layer_out = (after_attn.astype(jnp.float32) + mlp_sum.astype(jnp.float32)).astype(jnp.bfloat16)
        return layer_out, k_rot, v_heads

    return jax.shard_map(local_step, mesh=mesh, in_specs=arg_specs, out_specs=(row_spec, new_spec, new_spec), check_vma=False)
```

profile of v0, /device:TPU:0, one launch (start us, length us, event | category | flops | bytes accessed | tf_op | source)
XLA Modules:
  0.0 180.0 jit_solution(7225886811485823775)
XLA Ops:
  7.2 0.0 copy-start
  7.2 0.0 copy-start.1
  7.2 0.0 all-reduce.3.cloned.1.call-start
  7.3 0.8 convert_element_type.118
  8.1 1.4 convert_reduce_fusion.1
  9.5 1.5 fusion.15
  11.1 0.6 fusion.39
  11.7 0.0 copy-start.8
  11.7 0.6 slice_bitcast_fusion.1
  12.4 0.1 fusion.58
  12.5 1.0 multiply_cosine_fusion
  13.5 0.0 copy-done.10
  13.5 0.0 copy-done.8
  13.5 0.0 copy-done.16
  13.5 0.6 convolution_convert_fusion.2
  14.1 0.0 copy-done.18
  14.2 0.1 copy.18
  14.3 0.1 copy.19
  14.4 0.8 slice_bitcast_fusion
  15.3 1.5 iota_compare_fusion
  16.7 1.3 maximum_bitcast_fusion
  18.1 1.5 copy.23
  19.6 2.4 %fusion.68 = (f32[128,128]{1,0:T(8,128)}, bf16[128,128]{1,0:T(8,128)(2,1)}) fusion(bf16[3072,128]{1,0:T(8,128)(2,1)} %param.20, bf16[128,3072]{1,0:T(8,128)(2,1)S(1)} %copy-done.1, f32[3072]{0:T(1024)} %copy-done.10, f32[3072]{0:T(1024)} %copy-done.9, f32[128]{0:T(128)} %copy-done.18, f32[128]{0:T(128)} %copy-done.15), kind=kOutput, calls=%fused_computation.85 | convolution fusion | flops 103055360 | bytes 1696768 | tf_op jit(solution)/shard_map/dot_general | solution.py:74
  21.9 0.0 copy-done.5
  21.9 0.3 fusion.51
  22.2 0.3 pad_maximum_fusion
  22.6 0.0 copy-start.2
  22.6 0.9 fusion.71
  23.5 0.0 copy-done.2
  23.5 10.4 %fusion.67 = (f32[128,3]{1,0:T(8,128)S(1)}, f32[128,3,512]{2,1,0:T(4,128)S(1)}) fusion(bf16[128,3,128]{2,1,0:T(4,128)(2,1)} %copy-done.2, bf16[128,512,1,128]{3,1,2,0:T(8,128)(2,1)} %param.26, f32[128,3]{1,0:T(8,128)} %bitcast.54, pred[128,512]{1,0:T(8,128)(4,1)} %get-tuple-element.19, pred[128,512]{1,0:T(8,128)(4,1)S(1)} %get-tuple-element.20), kind=kOutput, calls=%fused_computation.84 | convolution fusion | flops 51315200 | bytes 17796096 | tf_op jit(solution)/shard_map/sub | solution.py:48
  33.9 0.7 convert_reduce_fusion.2
  34.5 0.2 copy-done.6
  34.7 7.2 %fusion.26 = bf16[128,3,128]{2,1,0:T(4,128)(2,1)S(1)} fusion(bf16[128,512,1,128]{3,1,2,0:T(8,128)(2,1)} %param.27, bf16[128,3,512]{2,1,0:T(4,128)(2,1)S(1)} %get-tuple-element.12, pred[128,512]{1,0:T(8,128)(4,1)S(1)} %get-tuple-element.20, f32[128,128]{1,0:T(8,128)S(1)} %copy-done.6, f32[128,3]{1,0:T(8,128)S(1)} %get-tuple-element.11), kind=kOutput, calls=%fused_computation.34 | convolution fusion | flops 50675712 | bytes 17401344 | tf_op jit(solution)/shard_map/rkgs,rskd->rkgd/dot_general | solution.py:52
  41.9 0.1 copy.21
  42.1 0.0 copy-start.13
  42.1 0.0 copy-start.14
  42.1 1.5 convolution_convert_fusion.1
  43.6 0.0 all-reduce.3.cloned.1.call-update
  43.6 0.2 all-reduce.5.cloned.1.call-start
  43.9 60.1 %all-reduce.3.cloned.1.call-done = bf16[128,3072]{1,0:T(8,128)(2,1)} async-done(((bf16[128,3072]{1,0:T(8,128)(2,1)}), bf16[128,3072]{1,0:T(8,128)(2,1)}) %all-reduce.3.cloned.1.call-update) | async-done | bytes 786448 | tf_op jit(solution)/shard_map/psum | solution.py:80
  104.0 1.7 convert_reduce_fusion
  105.7 0.4 fusion.11
  106.1 8.2 %convolution_convert_fusion = bf16[128,3072]{1,0:T(8,128)(2,1)} fusion(bf16[1152,3072]{1,0:T(8,128)(2,1)} %param.25, bf16[3072,1152]{1,0:T(8,128)(2,1)} %param.24, bf16[128,3072]{1,0:T(8,128)(2,1)S(1)} %get-tuple-element.10, f32[3072]{0:T(1024)S(1)} %convert_element_type.132, f32[3072]{0:T(1024)S(1)} %convert_add_fusion.2, f32[128]{0:T(128)S(1)} %add_rsqrt_fusion, ...), kind=kOutput, calls=%fused_computation.5 | convolution fusion | flops 1815134208 | bytes 15754240 | tf_op jit(solution)/shard_map/dot_general | solution.py:85
  114.3 0.0 all-reduce.5.cloned.1.call-update
  114.3 0.8 slice.49
  115.1 0.7 copy.22
  115.8 55.2 %all-reduce.5.cloned.1.call-done = bf16[128,3072]{1,0:T(8,128)(2,1)} async-done(((bf16[128,3072]{1,0:T(8,128)(2,1)}), bf16[128,3072]{1,0:T(8,128)(2,1)}) %all-reduce.5.cloned.1.call-update) | async-done | bytes 786448 | tf_op jit(solution)/shard_map/psum | solution.py:86
  170.9 2.2 %fusion.20 = bf16[128,3072]{1,0:T(8,128)(2,1)} fusion(bf16[128,3072]{1,0:T(8,128)(2,1)S(1)} %get-tuple-element.10, bf16[128,3072]{1,0:T(8,128)(2,1)} %all-reduce.5.cloned.1.call-done), kind=kLoop, calls=%fused_computation.29 | loop fusion | flops 1572864 | bytes 2359296 | tf_op jit(solution)/shard_map/convert_element_type | solution.py:87
  (36 shorter events, 0.1 us)
Async XLA Ops:
  7.2 34.9 %copy-start = (bf16[384,3072]{1,0:T(8,128)(2,1)S(1)}, bf16[384,3072]{1,0:T(8,128)(2,1)}, u32[]{:S(2)}) copy-start(bf16[384,3072]{1,0:T(8,128)(2,1)} %param.21) | copy-start | bytes 7077892
  7.2 3.9 %copy-start.1 = (bf16[128,3072]{1,0:T(8,128)(2,1)S(1)}, bf16[128,3072]{1,0:T(8,128)(2,1)}, u32[]{:S(2)}) copy-start(bf16[128,3072]{1,0:T(8,128)(2,1)} %param.14) | copy-start | bytes 2359300
  7.2 3.8 %copy-start.11 = (bf16[3072]{0:T(1024)(128)(2,1)S(1)}, bf16[3072]{0:T(1024)(128)(2,1)}, u32[]{:S(2)}) copy-start(bf16[3072]{0:T(1024)(128)(2,1)} %param.16) | copy-start | bytes 18436
  7.2 3.9 %copy-start.12 = (bf16[3072]{0:T(1024)(128)(2,1)S(1)}, bf16[3072]{0:T(1024)(128)(2,1)}, u32[]{:S(2)}) copy-start(bf16[3072]{0:T(1024)(128)(2,1)} %param.17) | copy-start | bytes 18436
  7.2 96.8 %all-reduce.3.cloned.1.call-start = ((), (), s32[]{:S(2)}) async-start(), calls=%async_computation | async-start | bytes 1572864 | tf_op jit(solution)/shard_map/psum | solution.py:80
  7.3 3.8 %copy-start.17 = (bf16[3072,128]{1,0:T(8,128)(2,1)S(1)}, bf16[3072,128]{1,0:T(8,128)(2,1)}, u32[]{:S(2)}) copy-start(bf16[3072,128]{1,0:T(8,128)(2,1)} %param.19) | copy-start | bytes 2359300
  9.5 4.0 %copy-start.15 = (f32[128]{0:T(128)}, f32[128]{0:T(128)S(1)}, u32[]{:S(2)}) copy-start(f32[128]{0:T(128)S(1)} %broadcast_multiply_fusion.1) | copy-start | bytes 1540
  11.0 2.5 %copy-start.16 = (bf16[3072,384]{1,0:T(8,128)(2,1)S(1)}, bf16[3072,384]{1,0:T(8,128)(2,1)}, u32[]{:S(2)}) copy-start(bf16[3072,384]{1,0:T(8,128)(2,1)} %param.18) | copy-start | bytes 7077892
  11.0 3.1 %copy-start.18 = (f32[128]{0:T(128)}, f32[128]{0:T(128)S(1)}, u32[]{:S(2)}) copy-start(f32[128]{0:T(128)S(1)} %add_rsqrt_fusion.1) | copy-start | bytes 1540
  11.1 2.4 %copy-start.9 = (f32[3072]{0:T(1024)}, f32[3072]{0:T(1024)S(1)}, u32[]{:S(2)}) copy-start(f32[3072]{0:T(1024)S(1)} %convert_add_fusion.3) | copy-start | bytes 36868
  11.1 2.4 %copy-start.10 = (f32[3072]{0:T(1024)}, f32[3072]{0:T(1024)S(1)}, u32[]{:S(2)}) copy-start(f32[3072]{0:T(1024)S(1)} %convert_element_type.113) | copy-start | bytes 36868
  11.7 1.8 copy-start.8
  15.3 6.7 %copy-start.4 = (f32[128,32]{1,0:T(8,128)S(1)}, f32[128,32]{1,0:T(8,128)}, u32[]{:S(2)}) copy-start(f32[128,32]{1,0:T(8,128)} %get-tuple-element.17) | copy-start | bytes 49156
  19.6 2.4 %copy-start.5 = (f32[128,32]{1,0:T(8,128)S(1)}, f32[128,32]{1,0:T(8,128)}, u32[]{:S(2)}) copy-start(f32[128,32]{1,0:T(8,128)} %get-tuple-element.18) | copy-start | bytes 49156
  19.6 2.7 %copy-start.3 = (bf16[128,3,64]{2,1,0:T(4,128)(2,1)S(1)}, bf16[128,3,64]{2,1,0:T(4,128)(2,1)}, u32[]{:S(2)}) copy-start(bf16[128,3,64]{2,1,0:T(4,128)(2,1)} %slice_bitcast_fusion) | copy-start | bytes 147460
  19.6 3.0 %copy-start.7 = (bf16[128,128,1]{1,2,0:T(2,128)(2,1)S(1)}, bf16[128,128,1]{1,2,0:T(2,128)(2,1)}, u32[]{:S(2)}) copy-start(bf16[128,128,1]{1,2,0:T(2,128)(2,1)} %copy.23) | copy-start | bytes 98308
  22.6 0.9 copy-start.2
  33.9 0.8 copy-start.6
  42.1 1.8 copy-start.13
  42.1 1.8 copy-start.14
  43.6 127.3 %all-reduce.5.cloned.1.call-start = ((), (), s32[]{:S(2)}) async-start(), calls=%async_computation.1 | async-start | bytes 1572864 | tf_op jit(solution)/shard_map/psum | solution.py:86
Sparse Core Ops, SparseCore 0:
  43.7 60.2 all-reduce.2
  114.4 56.4 all-reduce.4
where the time goes:
time: 180 us
  waiting for transfers between devices  115 us (64%)
  matrix products  31.8 us (18%)
  between operations  14.4 us (8%)
  other arithmetic  13.2 us (7%)
  local copies, waits for them, and re-layouts  5.09 us (3%)
    psum x1, waiting for transfers between devices, local_step(): attn_sum = lax.psum(attn_part, 'tp')  60.1 us
    psum x1, waiting for transfers between devices, local_step(): mlp_sum = lax.psum(mlp_part, 'tp')  55.2 us
    sub x1, matrix products, attend(): prob_map = jax.nn.softmax(scores, axis=-1).astype(jnp.bfloat16)  10.4 us
    dot_general x1, matrix products, local_step(): jnp.dot(activated, w_down, preferred_element_type=jnp.float32)  8.18 us
    dot_general x1, matrix products, attend(): jnp.einsum('rkgs,rskd->rkgd', old_probs, v_cache, preferred_element_type=...  7.2 us
  transfers between devices with their start and end apart: 2, of which 2 were waited for; matrix products, arithmetic and copies ran while one was open for 1% of the time, Pallas kernels for 0%

commit v1 on v0

--- a/solution.py
+++ b/solution.py
@@ -2,6 +2,8 @@
 import jax
 import jax.numpy as jnp
 from jax import lax
+from jax.experimental import pallas as pl
+from jax.experimental.pallas import tpu as pltpu
 from jax.sharding import PartitionSpec as P
 
 LN_EPS = 1e-5
@@ -54,6 +56,272 @@
     return context.astype(jnp.bfloat16).reshape(row_count, -1)
 
 
+MESH_ID = pl.DeviceIdType.MESH
+ROWS = 128
+OWN = 64
+MSG = 4
+MROWS = 16
+COLS = 3072
+CSPLIT = 2
+U1 = MSG * CSPLIT
+CW1 = COLS // CSPLIT
+U2 = 12
+CW2 = COLS // U2
+SKEW1 = 3
+SKEW2 = 4
+
+
+def tail_kernel(part_ref, res_ref, gain_ref, shift_ref, wup_hbm, wdn_hbm, out_hbm,
+                wup, wdn, d1, l1, c1, t1, x1, h2, act, p2, d2, l2, c2, t2, obuf,
+                w_sem, sd1, rd1, sl1, rl1, rc1, shp, rhp, she, rhe,
+                sd2, rd2, sl2, rl2, rc2, sop, rop, soe, roe, o_sem):
+    f32 = jnp.float32
+    bf16 = jnp.bfloat16
+    tp = lax.axis_index('tp')
+    core = lax.rem(tp, 2)
+    z = lax.div(tp, 2)
+    other = 1 - core
+    partner = tp + 1 - 2 * core
+    line = tp + 2 - 4 * lax.rem(z, 2)
+    cross = (3 - z) * 2 + core
+    mid = jnp.logical_or(z == 1, z == 2)
+    edge = jnp.logical_not(mid)
+
+    load_up = pltpu.make_async_copy(wup_hbm, wup, w_sem.at[0])
+    load_dn = pltpu.make_async_copy(wdn_hbm, wdn, w_sem.at[1])
+    load_up.start()
+    load_dn.start()
+
+    barrier = pltpu.get_barrier_semaphore()
+    pl.semaphore_signal(barrier, inc=1, device_id={'tp': partner}, device_id_type=MESH_ID)
+    pl.semaphore_signal(barrier, inc=1, device_id={'tp': line}, device_id_type=MESH_ID)
+
+    @pl.when(mid)
+    def _():
+        pl.semaphore_signal(barrier, inc=1, device_id={'tp': cross}, device_id_type=MESH_ID)
+        pl.semaphore_wait(barrier, 3)
+
+    @pl.when(edge)
+    def _():
+        pl.semaphore_wait(barrier, 2)
+
+    def send(src, dst, ssem, rsem, dev):
+        return pltpu.make_async_remote_copy(
+            src_ref=src, dst_ref=dst, send_sem=ssem, recv_sem=rsem,
+            device_id={'tp': dev}, device_id_type=MESH_ID)
+
+    def cut1(u):
+        return u // CSPLIT, pl.ds((u % CSPLIT) * CW1, CW1)
+
+    def rows_of(half, m):
+        return pl.ds(pl.multiple_of(half * OWN + m * MROWS, MROWS), MROWS)
+
+    def give1(u):
+        m, cs = cut1(u)
+        return send(part_ref.at[rows_of(other, m), cs], d1.at[m, :, cs], sd1.at[u], rd1.at[u], partner)
+
+    def line1(u):
+        m, cs = cut1(u)
+        return send(t1.at[m, :, cs], l1.at[m, :, cs], sl1.at[u], rl1.at[u], line)
+
+    def cross1(u):
+        m, cs = cut1(u)
+        return send(t1.at[m, :, cs], c1.at[m, :, cs], sl1.at[u], rc1.at[u], cross)
+
+    def share_h(m):
+        return send(h2.at[core, m], h2.at[core, m], shp.at[m], rhp.at[m], partner)
+
+    def push_h(m):
+        return send(h2.at[core, m], h2.at[core, m], she.at[m], rhe.at[m], line)
+
+    for u in range(U1):
+        give1(u).start()
+
+    def pair1(u):
+        m, cs = cut1(u)
+        give1(u).wait_recv()
+        return part_ref[rows_of(core, m), cs].astype(f32) + d1[m, :, cs].astype(f32)
+
+    def mid_add1(u):
+        m, cs = cut1(u)
+        pair = pair1(u)
+        line1(u).wait_recv()
+        t1[m, :, cs] = (pair + l1[m, :, cs].astype(f32)).astype(bf16)
+        cross1(u).start()
+
+    def mid_total1(u):
+        m, cs = cut1(u)
+        cross1(u).wait_recv()
+        total = (t1[m, :, cs].astype(f32) + c1[m, :, cs].astype(f32)).astype(bf16)
+        x1[m, :, cs] = (res_ref[rows_of(core, m), cs].astype(f32) + total.astype(f32)).astype(bf16)
+        if u % CSPLIT == CSPLIT - 1:
+            blk = x1[m].astype(f32)
+            mean = jnp.mean(blk, axis=-1, keepdims=True)
+            cent = blk - mean
+            var = jnp.mean(cent * cent, axis=-1, keepdims=True)
+            nrm = cent * lax.rsqrt(var + LN_EPS)
+            h2[core, m] = (nrm * (1.0 + gain_ref[...].astype(f32)) + shift_ref[...].astype(f32)).astype(bf16)
+            push_h(m).start()
+            share_h(m).start()
+
+    @pl.when(mid)
+    def _():
+        for s in range(U1 + SKEW1):
+            if s < U1:
+                mid_add1(s)
+            if s >= SKEW1:
+                mid_total1(s - SKEW1)
+
+    @pl.when(edge)
+    def _():
+        for u in range(U1):
+            m, cs = cut1(u)
+            t1[m, :, cs] = pair1(u).astype(bf16)
+            line1(u).start()
+        for m in range(MSG):
+            push_h(m).wait_recv()
+            share_h(m).start()
+
+    for m in range(MSG):
+        share_h(m).wait_recv()
+
+    load_up.wait()
+    nb = 384
+    hmat = h2[...].reshape(ROWS, COLS)
+    for n in range(wup.shape[1] // nb):
+        up = jnp.dot(hmat, wup[:, n * nb:(n + 1) * nb], preferred_element_type=f32)
+        act[:, n * nb:(n + 1) * nb] = jnp.square(jnp.maximum(up, 0.0)).astype(bf16)
+    load_dn.wait()
+
+    def give2(u):
+        return send(p2.at[u, other], d2.at[u], sd2.at[u], rd2.at[u], partner)
+
+    def line2(u):
+        return send(t2.at[u], l2.at[u], sl2.at[u], rl2.at[u], line)
+
+    def cross2(u):
+        return send(t2.at[u], c2.at[u], sl2.at[u], rc2.at[u], cross)
+
+    def share_o(u):
+        return send(obuf.at[u, core], obuf.at[u, core], sop.at[u], rop.at[u], partner)
+
+    def push_o(u):
+        return send(obuf.at[u, core], obuf.at[u, core], soe.at[u], roe.at[u], line)
+
+    def put_o(u, half):
+        return pltpu.make_async_copy(
+            obuf.at[u, half],
+            out_hbm.at[pl.ds(pl.multiple_of(half * OWN, OWN), OWN), pl.ds(u * CW2, CW2)],
+            o_sem.at[u, half])
+
+    def down(u):
+        dn = jnp.dot(act[...], wdn[:, u * CW2:(u + 1) * CW2], preferred_element_type=f32)
+        p2[u] = dn.astype(bf16).reshape(2, OWN, CW2)
+        give2(u).start()
+
+    def pair2(u):
+        give2(u).wait_recv()
+        return p2[u, core].astype(f32) + d2[u].astype(f32)
+
+    def mid_add2(u):
+        pair = pair2(u)
+        line2(u).wait_recv()
+        t2[u] = (pair + l2[u].astype(f32)).astype(bf16)
+        cross2(u).start()
+
+    def mid_total2(u):
+        cross2(u).wait_recv()
+        total = (t2[u].astype(f32) + c2[u].astype(f32)).astype(bf16)
+        own = x1[:, :, u * CW2:(u + 1) * CW2].reshape(OWN, CW2)
+        obuf[u, core] = (own.astype(f32) + total.astype(f32)).astype(bf16)
+        push_o(u).start()
+        share_o(u).start()
+        put_o(u, core).start()
+
+    @pl.when(mid)
+    def _():
+        down(0)
+        down(1)
+        for s in range(U2 + SKEW2):
+            if s + 2 < U2:
+                down(s + 2)
+            if s < U2:
+                mid_add2(s)
+            if s >= SKEW2:
+                mid_total2(s - SKEW2)
+
+    @pl.when(edge)
+    def _():
+        down(0)
+        down(1)
+        for u in range(U2):
+            if u + 2 < U2:
+                down(u + 2)
+            t2[u] = pair2(u).astype(bf16)
+            line2(u).start()
+        for u in range(U2):
+            push_o(u).wait_recv()
+            share_o(u).start()
+            put_o(u, core).start()
+
+    for u in range(U2):
+        share_o(u).wait_recv()
+        put_o(u, other).start()
+
+    for u in range(U1):
+        give1(u).wait_send()
+        line1(u).wait_send()
+    for m in range(MSG):
+        share_h(m).wait_send()
+    for u in range(U2):
+        give2(u).wait_send()
+        line2(u).wait_send()
+        share_o(u).wait_send()
+        put_o(u, core).wait()
+        put_o(u, other).wait()
+
+    @pl.when(mid)
+    def _():
+        for m in range(MSG):
+            push_h(m).wait_send()
+        for u in range(U2):
+            push_o(u).wait_send()
+
+
+def tail_call(part, residual, gain, shift, w_up, w_down):
+    bf16 = jnp.bfloat16
+    ff = w_up.shape[1]
+    vm = pl.BlockSpec(memory_space=pltpu.VMEM)
+    hb = pl.BlockSpec(memory_space=pl.ANY)
+    dma = pltpu.SemaphoreType.DMA
+    return pl.pallas_call(
+        tail_kernel,
+        name='tail',
+        out_shape=jax.ShapeDtypeStruct((ROWS, COLS), bf16),
+        in_specs=[vm, vm, vm, vm, hb, hb],
+        out_specs=hb,
+        scratch_shapes=[
+            pltpu.VMEM((COLS, ff), bf16), pltpu.VMEM((ff, COLS), bf16),
+            pltpu.VMEM((MSG, MROWS, COLS), bf16), pltpu.VMEM((MSG, MROWS, COLS), bf16),
+            pltpu.VMEM((MSG, MROWS, COLS), bf16), pltpu.VMEM((MSG, MROWS, COLS), bf16),
+            pltpu.VMEM((MSG, MROWS, COLS), bf16),
+            pltpu.VMEM((2, MSG, MROWS, COLS), bf16),
+            pltpu.VMEM((ROWS, ff), bf16),
+            pltpu.VMEM((U2, 2, OWN, CW2), bf16),
+            pltpu.VMEM((U2, OWN, CW2), bf16), pltpu.VMEM((U2, OWN, CW2), bf16),
+            pltpu.VMEM((U2, OWN, CW2), bf16), pltpu.VMEM((U2, OWN, CW2), bf16),
+            pltpu.VMEM((U2, 2, OWN, CW2), bf16),
+            dma((2,)),
+            dma((U1,)), dma((U1,)), dma((U1,)), dma((U1,)), dma((U1,)),
+            dma((MSG,)), dma((MSG,)), dma((MSG,)), dma((MSG,)),
+            dma((U2,)), dma((U2,)), dma((U2,)), dma((U2,)), dma((U2,)),
+            dma((U2,)), dma((U2,)), dma((U2,)), dma((U2,)),
+            dma((U2, 2)),
+        ],
+        compiler_params=pltpu.CompilerParams(collective_id=0, has_side_effects=True, vmem_limit_bytes=50 * 1024 * 1024),
+    )(part, residual, gain, shift, w_up, w_down)
+
+
 def solution(mesh):
     row_spec = P('dp', None)
     whole_spec = P()
@@ -77,14 +345,7 @@
         v_heads = v_proj.reshape(row_count, slots_here, head_dim)
         context = attend(q_rot, k_rot, v_heads, k_cache, v_cache, positions)
         attn_part = jnp.dot(context, w_o, preferred_element_type=jnp.float32).astype(jnp.bfloat16)
-        attn_sum = lax.psum(attn_part, 'tp')
-        after_attn = (residual.astype(jnp.float32) + attn_sum.astype(jnp.float32)).astype(jnp.bfloat16)
-        normed_mid = layer_norm_1p(after_attn, ln2_gain, ln2_shift)
-        up_proj = jnp.dot(normed_mid, w_up, preferred_element_type=jnp.float32)
-        activated = jnp.square(jnp.maximum(up_proj, 0.0)).astype(jnp.bfloat16)
-        mlp_part = jnp.dot(activated, w_down, preferred_element_type=jnp.float32).astype(jnp.bfloat16)
-        mlp_sum = lax.psum(mlp_part, 'tp')
-        layer_out = (after_attn.astype(jnp.float32) + mlp_sum.astype(jnp.float32)).astype(jnp.bfloat16)
+        layer_out = tail_call(attn_part, residual, ln2_gain[None, :], ln2_shift[None, :], w_up, w_down)
         return layer_out, k_rot, v_heads
 
     return jax.shard_map(local_step, mesh=mesh, in_specs=arg_specs, out_specs=(row_spec, new_spec, new_spec), check_vma=False)

time: 180 us -> 83 us (0.46)
  waiting for transfers between devices: 115 us -> 0 us
  Pallas kernels: 0 us -> 45.6 us
  between operations: 14.4 us -> 1.04 us
  matrix products: 31.8 us -> 23.4 us
  other arithmetic: 13.2 us -> 6.83 us
    psum x2 -> x0, waiting for transfers between devices: 115 us -> none  [the longest x1 60.1 us: local_step(): attn_sum = lax.psum(attn_part, 'tp')]
    pallas_call x0 -> x1, Pallas kernels: none -> 45.6 us  [tail_call(): pl.pallas_call(tail_kernel, name='tail', out_shape=jax.ShapeDtypeStruct((...]
    dot_general x1 -> x0, matrix products: 8.18 us -> none  [local_step(): jnp.dot(activated, w_down, preferred_element_type=jnp.float32)]
    unnamed x39 -> x40, local copies, waits for them, and re-layouts: 1 us -> 4.27 us
    concatenate x3, local copies, waits for them, and re-layouts: 2.93 us -> 0.26 us  [rotate_first_half(): jnp.concatenate([first_half * cos_table - second_half * sin_table, second...]
    convert_element_type x1 -> x0, other arithmetic: 2.2 us -> none  [local_step(): (after_attn.astype(jnp.float32) + mlp_sum.astype(jnp.float32)).astype(jnp...]
  transfers between devices with their start and end apart: 2 -> 0, of which waited for: 2 -> 0; matrix products, arithmetic and copies ran while one was open for 1% -> 0% of each run, Pallas kernels for 0% -> 0%
where the time goes in v1:
time: 83 us; the launch traced here: 82.5 us
  Pallas kernels  45.6 us (55%)
  matrix products  23.4 us (28%)
  other arithmetic  6.83 us (8%)
  local copies, waits for them, and re-layouts  5.71 us (7%)
  between operations  1.04 us (1%)
    pallas_call x1, Pallas kernels, tail_call(): pl.pallas_call(tail_kernel, name='tail', out_shape=jax.ShapeDtypeStruct((...  45.6 us
    sub x1, matrix products, attend(): prob_map = jax.nn.softmax(scores, axis=-1).astype(jnp.bfloat16)  11.3 us
    dot_general x1, matrix products, attend(): jnp.einsum('rkgs,rskd->rkgd', old_probs, v_cache, preferred_element_type=...  7.2 us
    unnamed x40, local copies, waits for them, and re-layouts  4.27 us
    dot_general x1, matrix products, local_step(): jnp.dot(normed, w_q, preferred_element_type=jnp.float32)  2.3 us
    reduce_sum x1, other arithmetic, attend(): jnp.sum(jnp.where(at_pos, prob_map, zero_bf).astype(jnp.float32), axis=-1)  1.95 us

profile of v1, /device:TPU:0, one launch (start us, length us, event | category | flops | bytes accessed | tf_op | source)
XLA Modules:
  0.0 82.5 jit_solution(10962269876305751653)
XLA Ops:
  0.6 0.0 copy-start
  0.6 0.0 copy-start.1
  0.7 0.0 copy-start.8
  0.7 0.0 copy-start.9
  0.7 1.5 %convert_reduce_fusion = f32[128]{0:T(128)S(1)} fusion(bf16[128,3072]{1,0:T(8,128)(2,1)} %res_ref.1), kind=kLoop, calls=%fused_computation.7 | loop fusion | flops 786304 | bytes 786944 | tf_op jit(solution)/shard_map/reduce_sum | solution.py:15
  2.2 1.5 %fusion.7 = f32[128]{0:T(128)S(1)} fusion(bf16[128,3072]{1,0:T(8,128)(2,1)} %res_ref.1, f32[128]{0:T(128)S(1)} %broadcast_multiply_fusion), kind=kLoop, calls=%fused_computation.10 | loop fusion | flops 1572736 | bytes 787456 | tf_op jit(solution)/shard_map/reduce_sum | solution.py:17
  3.7 0.0 copy-done.8
  3.7 0.0 copy-start.17
  3.7 0.0 copy-done.9
  3.7 0.0 copy-start.4
  3.7 0.0 copy-done.1
  3.7 0.0 copy-start.6
  3.8 0.0 copy-start.12
  3.8 2.3 %convolution_convert_fusion.1 = bf16[128,384]{1,0:T(8,128)(2,1)S(1)} fusion(bf16[3072,384]{1,0:T(8,128)(2,1)} %param.18, bf16[128,3072]{1,0:T(8,128)(2,1)S(1)} %copy-done.1, f32[3072]{0:T(1024)S(1)} %convert_element_type.81, f32[3072]{0:T(1024)S(1)} %convert_add_fusion, f32[128]{0:T(128)S(1)} %add_rsqrt_fusion, f32[128]{0:T(128)S(1)} %broadcast_multiply_fusion), kind=kOutput, calls=%fused_computation.16 | convolution fusion | flops 304398336 | bytes 3269632 | tf_op jit(solution)/shard_map/dot_general | solution.py:340
  6.1 0.1 copy.18
  6.2 0.1 copy.19
  6.3 0.0 copy-start.15
  6.4 0.0 copy-done.12
  6.4 0.3 multiply_cosine_fusion
  6.7 0.3 fusion.33
  7.0 0.1 slice_bitcast_fusion
  7.2 0.3 pad_maximum_fusion
  7.5 0.0 copy-done.13
  7.5 0.0 copy-done.17
  7.5 0.0 copy-done.4
  7.5 0.6 fusion.29
  8.1 0.0 copy-start.3
  8.1 0.1 fusion.40
  8.3 0.5 copy-done.3
  8.8 0.1 copy.23
  8.9 0.3 fusion.51
  9.2 0.8 iota_compare_fusion
  10.0 11.3 %fusion.47 = (f32[128,3]{1,0:T(8,128)S(1)}, f32[128,3,512]{2,1,0:T(4,128)}) fusion(bf16[128,3,128]{2,1,0:T(4,128)(2,1)S(1)} %pad_maximum_fusion, bf16[128,512,1,128]{3,1,2,0:T(8,128)(2,1)} %param.26, f32[128,3]{1,0:T(8,128)S(1)} %bitcast.52, pred[128,512]{1,0:T(8,128)(4,1)S(1)} %get-tuple-element.17, pred[128,512]{1,0:T(8,128)(4,1)S(1)} %get-tuple-element.18), kind=kOutput, calls=%fused_computation.59 | convolution fusion | flops 51315200 | bytes 17796096 | tf_op jit(solution)/shard_map/sub | solution.py:50
  21.3 2.0 %convert_reduce_fusion.1 = (f32[128,3]{1,0:T(8,128)S(1)}, bf16[128,3,512]{2,1,0:T(4,128)(2,1)S(1)}) fusion(pred[128,512]{1,0:T(8,128)(4,1)S(1)} %get-tuple-element.18, f32[128,3,512]{2,1,0:T(4,128)} %get-tuple-element.20, f32[128,3]{1,0:T(8,128)S(1)} %get-tuple-element.19), kind=kLoop, calls=%fused_computation.26 | loop fusion | flops 982656 | bytes 1248256 | tf_op jit(solution)/shard_map/reduce_sum | solution.py:53
  23.2 0.0 copy-done.5
  23.3 1.1 %fusion.48 = (f32[128,128]{1,0:T(8,128)S(1)}, bf16[128,128]{1,0:T(8,128)(2,1)}) fusion(bf16[3072,128]{1,0:T(8,128)(2,1)S(1)} %copy-done.16, bf16[128,3072]{1,0:T(8,128)(2,1)S(1)} %copy-done.1, f32[3072]{0:T(1024)S(1)} %copy-done.7, f32[3072]{0:T(1024)S(1)} %copy-done.5, f32[128]{0:T(128)S(1)} %copy-done.18, f32[128]{0:T(128)S(1)} %copy-done.14), kind=kOutput, calls=%fused_computation.60 | convolution fusion | flops 103055360 | bytes 1696768 | tf_op jit(solution)/shard_map/dot_general | solution.py:342
  24.4 7.2 %fusion.16 = bf16[128,3,128]{2,1,0:T(4,128)(2,1)S(1)} fusion(bf16[128,512,1,128]{3,1,2,0:T(8,128)(2,1)} %param.27, bf16[128,3,512]{2,1,0:T(4,128)(2,1)S(1)} %get-tuple-element.10, pred[128,512]{1,0:T(8,128)(4,1)S(1)} %get-tuple-element.18, f32[128,128]{1,0:T(8,128)S(1)} %get-tuple-element.21, f32[128,3]{1,0:T(8,128)S(1)} %get-tuple-element.9), kind=kOutput, calls=%fused_computation.18 | convolution fusion | flops 50675712 | bytes 17401344 | tf_op jit(solution)/shard_map/rkgs,rskd->rkgd/dot_general | solution.py:54
  31.6 0.1 copy.21
  31.8 0.0 copy-start.10
  31.8 0.0 copy-start.11
  31.8 0.6 convolution_convert_fusion.part_ref
  32.4 0.1 copy-done.10
  32.5 0.0 copy-done.11
  32.5 45.6 %tail.1 = bf16[128,3072]{1,0:T(8,128)(2,1)S(1)} custom-call(bf16[128,3072]{1,0:T(8,128)(2,1)S(1)} %convolution_convert_fusion.part_ref, bf16[128,3072]{1,0:T(8,128)(2,1)S(1)} %copy-done.1, bf16[1,3072]{1,0:T(2,128)(2,1)S(1)} %broadcast_in_dim.55.gain_ref, bf16[1,3072]{1,0:T(2,128)(2,1)S(1)} %broadcast_in_dim.76.shift_ref, bf16[3072,1152]{1,0:T(8,128)(2,1)} %wup_hbm.1, ...), custom_call_target="tpu_custom_call" | custom-call | tf_op jit(solution)/shard_map/tail/pallas_call | solution.py:297
  78.1 0.9 %copy-done.2 = bf16[128,3072]{1,0:T(8,128)(2,1)} copy-done((bf16[128,3072]{1,0:T(8,128)(2,1)}, bf16[128,3072]{1,0:T(8,128)(2,1)S(1)}, u32[]{:S(2)}) %copy-start.2) | copy-done | bytes 786456
  79.0 0.8 slice.49
  79.8 0.7 copy.22
  80.5 2.1 %copy.26 = bf16[128,3072]{1,0:T(8,128)(2,1)} copy(bf16[128,3072]{1,0:T(8,128)(2,1)} %copy-done.2) | data formatting | bytes 1572864
  (26 shorter events, 0.1 us)
Async XLA Ops:
  0.6 31.2 %copy-start = (bf16[384,3072]{1,0:T(8,128)(2,1)S(1)}, bf16[384,3072]{1,0:T(8,128)(2,1)}, u32[]{:S(2)}) copy-start(bf16[384,3072]{1,0:T(8,128)(2,1)} %param.21) | copy-start | bytes 7077892
  0.6 3.1 %copy-start.1 = (bf16[128,3072]{1,0:T(8,128)(2,1)S(1)}, bf16[128,3072]{1,0:T(8,128)(2,1)}, u32[]{:S(2)}) copy-start(bf16[128,3072]{1,0:T(8,128)(2,1)} %res_ref.1) | copy-start | bytes 2359300
  0.7 3.0 %copy-start.8 = (bf16[3072]{0:T(1024)(128)(2,1)S(1)}, bf16[3072]{0:T(1024)(128)(2,1)}, u32[]{:S(2)}) copy-start(bf16[3072]{0:T(1024)(128)(2,1)} %param.16) | copy-start | bytes 18436
  0.7 3.0 %copy-start.9 = (bf16[3072]{0:T(1024)(128)(2,1)S(1)}, bf16[3072]{0:T(1024)(128)(2,1)}, u32[]{:S(2)}) copy-start(bf16[3072]{0:T(1024)(128)(2,1)} %param.17) | copy-start | bytes 18436
  2.2 5.3 %copy-start.13 = (f32[128]{0:T(128)}, f32[128]{0:T(128)S(1)}, u32[]{:S(2)}) copy-start(f32[128]{0:T(128)S(1)} %broadcast_multiply_fusion) | copy-start | bytes 1540
  3.7 3.8 %copy-start.17 = (f32[128]{0:T(128)}, f32[128]{0:T(128)S(1)}, u32[]{:S(2)}) copy-start(f32[128]{0:T(128)S(1)} %add_rsqrt_fusion) | copy-start | bytes 1540
  3.7 3.8 %copy-start.4 = (f32[3072]{0:T(1024)}, f32[3072]{0:T(1024)S(1)}, u32[]{:S(2)}) copy-start(f32[3072]{0:T(1024)S(1)} %convert_add_fusion) | copy-start | bytes 36868
  3.7 3.8 %copy-start.6 = (f32[3072]{0:T(1024)}, f32[3072]{0:T(1024)S(1)}, u32[]{:S(2)}) copy-start(f32[3072]{0:T(1024)S(1)} %convert_element_type.81) | copy-start | bytes 36868
  3.8 2.7 %copy-start.12 = (s32[128]{0:T(128)S(1)}, s32[128]{0:T(128)}, u32[]{:S(2)}) copy-start(s32[128]{0:T(128)} %param.15) | copy-start | bytes 1540
  6.3 1.2 %copy-start.15 = (bf16[3072,128]{1,0:T(8,128)(2,1)S(1)}, bf16[3072,128]{1,0:T(8,128)(2,1)}, u32[]{:S(2)}) copy-start(bf16[3072,128]{1,0:T(8,128)(2,1)} %param.19) | copy-start | bytes 2359300
  8.1 0.6 copy-start.3
  21.3 2.0 %copy-start.5 = (f32[3072]{0:T(1024)S(1)}, f32[3072]{0:T(1024)}, u32[]{:S(2)}) copy-start(f32[3072]{0:T(1024)} %copy-done.4) | copy-start | bytes 36868
  21.3 2.0 %copy-start.7 = (f32[3072]{0:T(1024)S(1)}, f32[3072]{0:T(1024)}, u32[]{:S(2)}) copy-start(f32[3072]{0:T(1024)} %copy-done.6) | copy-start | bytes 36868
  21.3 2.0 %copy-start.14 = (f32[128]{0:T(128)S(1)}, f32[128]{0:T(128)}, u32[]{:S(2)}) copy-start(f32[128]{0:T(128)} %copy-done.13) | copy-start | bytes 1540
  21.3 2.0 %copy-start.16 = (bf16[3072,128]{1,0:T(8,128)(2,1)S(1)}, bf16[3072,128]{1,0:T(8,128)(2,1)}, u32[]{:S(2)}) copy-start(bf16[3072,128]{1,0:T(8,128)(2,1)} %param.20) | copy-start | bytes 2359300
  21.3 2.0 %copy-start.18 = (f32[128]{0:T(128)S(1)}, f32[128]{0:T(128)}, u32[]{:S(2)}) copy-start(f32[128]{0:T(128)} %copy-done.17) | copy-start | bytes 1540
  31.8 0.7 copy-start.10
  31.8 0.7 copy-start.11
  78.1 0.9 %copy-start.2 = (bf16[128,3072]{1,0:T(8,128)(2,1)}, bf16[128,3072]{1,0:T(8,128)(2,1)S(1)}, u32[]{:S(2)}) copy-start(bf16[128,3072]{1,0:T(8,128)(2,1)S(1)} %tail.1) | copy-start | bytes 2359300

commit v2 on v1

--- a/solution.py
+++ b/solution.py
@@ -8,52 +8,6 @@
 
 LN_EPS = 1e-5
 ROPE_BASE = 10000.0
-
-
-def layer_norm_1p(row_block, gain_vec, shift_vec):
-    block32 = row_block.astype(jnp.float32)
-    row_mean = jnp.mean(block32, axis=-1, keepdims=True)
-    centered = block32 - row_mean
-    row_var = jnp.mean(centered * centered, axis=-1, keepdims=True)
-    normed = centered * lax.rsqrt(row_var + LN_EPS)
-    scaled = normed * (1.0 + gain_vec.astype(jnp.float32)) + shift_vec.astype(jnp.float32)
-    return scaled.astype(jnp.bfloat16)
-
-
-def rotate_first_half(head_vecs, positions):
-    head_dim = head_vecs.shape[-1]
-    rot_dim = head_dim // 2
-    half_rot = rot_dim // 2
-    inv_freq = jnp.power(ROPE_BASE, -2.0 * jnp.arange(half_rot, dtype=jnp.float32) / rot_dim)
-    angles = positions.astype(jnp.float32)[:, None] * inv_freq[None, :]
-    table_shape = (head_vecs.shape[0],) + (1,) * (head_vecs.ndim - 2) + (half_rot,)
-    cos_table = jnp.cos(angles).reshape(table_shape)
-    sin_table = jnp.sin(angles).reshape(table_shape)
-    vecs32 = head_vecs.astype(jnp.float32)
-    first_half = vecs32[..., :half_rot]
-    second_half = vecs32[..., half_rot:rot_dim]
-    turned = jnp.concatenate([first_half * cos_table - second_half * sin_table, second_half * cos_table + first_half * sin_table, vecs32[..., rot_dim:]], axis=-1)
-    return turned.astype(jnp.bfloat16)
-
-
-def attend(q_rot, k_rot, v_heads, k_cache, v_cache, positions):
-    row_count = k_cache.shape[0]
-    seq_max = k_cache.shape[1]
-    score_scale = 1.0 / math.sqrt(k_cache.shape[3])
-    old_scores = jnp.einsum('rkgd,rskd->rkgs', q_rot, k_cache, preferred_element_type=jnp.float32)
-    new_scores = jnp.einsum('rkgd,rkd->rkg', q_rot, k_rot, preferred_element_type=jnp.float32)
-    seq_index = jnp.arange(seq_max)[None, :]
-    at_pos = (seq_index == positions[:, None])[:, None, None, :]
-    valid_mask = (seq_index <= positions[:, None])[:, None, None, :]
-    scores = jnp.where(at_pos, new_scores[..., None], old_scores) * score_scale
-    scores = jnp.where(valid_mask, scores, -jnp.inf)
-    prob_map = jax.nn.softmax(scores, axis=-1).astype(jnp.bfloat16)
-    zero_bf = jnp.zeros((), jnp.bfloat16)
-    old_probs = jnp.where(at_pos, zero_bf, prob_map)
-    new_prob = jnp.sum(jnp.where(at_pos, prob_map, zero_bf).astype(jnp.float32), axis=-1)
-    context = jnp.einsum('rkgs,rskd->rkgd', old_probs, v_cache, preferred_element_type=jnp.float32)
-    context = context + new_prob[..., None] * v_heads.astype(jnp.float32)[:, :, None, :]
-    return context.astype(jnp.bfloat16).reshape(row_count, -1)
 
 
 MESH_ID = pl.DeviceIdType.MESH
@@ -322,6 +276,180 @@
     )(part, residual, gain, shift, w_up, w_down)
 
 
+HDIM = 128
+SEQ = 512
+GRP = 32
+NGRP = ROWS // GRP
+SUB = 8
+NSUB = GRP // SUB
+ROT = 64
+
+
+def head_kernel(x_hbm, pos_ref, gain_ref, shift_ref, wq_hbm, wk_hbm, wv_hbm, wo_hbm, k_hbm, v_hbm,
+                part_ref, knew_ref, vnew_ref,
+                xs, hs, wqkv, wo, kb, vb, qs, ks, vs, ps, cs, ss,
+                in_sem, w_sem, k_sem, v_sem):
+    f32 = jnp.float32
+    bf16 = jnp.bfloat16
+    nq = wq_hbm.shape[1]
+
+    load_x = pltpu.make_async_copy(x_hbm, xs, in_sem.at[0])
+    load_q = pltpu.make_async_copy(wq_hbm, wqkv.at[:, pl.ds(0, nq)], w_sem.at[0])
+    load_k = pltpu.make_async_copy(wk_hbm, wqkv.at[:, pl.ds(nq, HDIM)], w_sem.at[1])
+    load_v = pltpu.make_async_copy(wv_hbm, wqkv.at[:, pl.ds(nq + HDIM, HDIM)], w_sem.at[2])
+    load_o = pltpu.make_async_copy(wo_hbm, wo, in_sem.at[1])
+
+    def key_copy(g, s):
+        at = pl.ds(g * GRP + s * SUB, SUB)
+        return pltpu.make_async_copy(k_hbm.at[at], kb.at[at], k_sem.at[g, s])
+
+    def val_copy(g, s):
+        at = pl.ds(g * GRP + s * SUB, SUB)
+        return pltpu.make_async_copy(v_hbm.at[at], vb.at[at], v_sem.at[g, s])
+
+    load_x.start()
+    load_q.start()
+    load_k.start()
+    load_v.start()
+    for g in range(NGRP):
+        for s in range(NSUB):
+            key_copy(g, s).start()
+        if g == NGRP - 1:
+            load_o.start()
+        for s in range(NSUB):
+            val_copy(g, s).start()
+
+    lane = lax.broadcasted_iota(jnp.int32, (ROWS, HDIM), 1)
+    pos_col = jnp.transpose(jnp.broadcast_to(pos_ref[...].astype(f32), (ROWS, ROWS)))
+    half = ROT // 2
+    pair = lax.rem(lane, half).astype(f32)
+    inv = jnp.exp(pair * (-2.0 * math.log(ROPE_BASE) / ROT))
+    ang = pos_col * inv
+    in_rot = lane < ROT
+    cos_t = jnp.where(in_rot, jnp.cos(ang), 1.0)
+    sin_a = jnp.sin(ang)
+    sin_t = jnp.where(in_rot, jnp.where(lane < half, -sin_a, sin_a), 0.0)
+
+    def rotate(v):
+        swap = jnp.where(lane < half, pltpu.roll(v, HDIM - half, 1), pltpu.roll(v, half, 1))
+        return (v * cos_t + swap * sin_t).astype(bf16)
+
+    load_x.wait()
+    rb = 32
+    gain1 = 1.0 + gain_ref[...].astype(f32)
+    shift1 = shift_ref[...].astype(f32)
+    for r in range(ROWS // rb):
+        blk = xs[r * rb:(r + 1) * rb, :].astype(f32)
+        mean = jnp.mean(blk, axis=-1, keepdims=True)
+        cent = blk - mean
+        var = jnp.mean(cent * cent, axis=-1, keepdims=True)
+        nrm = cent * lax.rsqrt(var + LN_EPS)
+        hs[r * rb:(r + 1) * rb, :] = (nrm * gain1 + shift1).astype(bf16)
+
+    load_q.wait()
+    load_k.wait()
+    load_v.wait()
+    qkv = jnp.dot(hs[...], wqkv[...], preferred_element_type=f32).astype(bf16).astype(f32)
+    k_rot = rotate(qkv[:, nq:nq + HDIM])
+    v_head = qkv[:, nq + HDIM:nq + 2 * HDIM]
+    knew_ref[...] = k_rot
+    vnew_ref[...] = v_head.astype(bf16)
+    heads = nq // HDIM
+    for g in range(4):
+        at = pl.ds(g, ROWS, stride=4)
+        if g < heads:
+            qs[at, :] = rotate(qkv[:, g * HDIM:(g + 1) * HDIM]).astype(f32)
+        else:
+            qs[at, :] = jnp.zeros((ROWS, HDIM), f32)
+        ks[at, :] = k_rot.astype(f32)
+        vs[at, :] = v_head
+        ps[at, :] = pos_col
+
+    scale = 1.0 / math.sqrt(HDIM)
+    lane_b = lax.div(lane, 4)
+    row_i = lax.div(lax.broadcasted_iota(jnp.int32, (16, HDIM), 0), 4)
+    step_t = lax.broadcasted_iota(jnp.int32, (SEQ, HDIM), 0)
+
+    def group(g, carry):
+        rows = pl.ds(pl.multiple_of(g * (GRP * 4), GRP * 4), GRP * 4)
+        qg = qs[rows, :]
+        q_t = jnp.transpose(qg)
+        p_row = jnp.transpose(ps[rows, :])[0:1, :].astype(jnp.int32)
+        new_col = jnp.sum(qg * ks[rows, :], axis=-1, keepdims=True)
+        new_row = jnp.transpose(jnp.broadcast_to(new_col, (HDIM, HDIM)))[0:1, :]
+        for s in range(NSUB):
+            key_copy(g, s).wait()
+            base = g * GRP + s * SUB
+            left = jnp.concatenate([kb[base + i] for i in range(SUB)], axis=1)
+            right = jnp.concatenate(
+                [jnp.where(lane_b == s * SUB + i, q_t, 0.0).astype(bf16) for i in range(SUB)], axis=0)
+            acc = jnp.dot(left, right, preferred_element_type=f32)
+            if s == 0:
+                ss[...] = acc
+            else:
+                ss[...] += acc
+        is_new = step_t == p_row
+        sc = jnp.where(is_new, new_row, ss[...]) * scale
+        sc = jnp.where(step_t <= p_row, sc, -jnp.inf)
+        top = jnp.max(sc, axis=0, keepdims=True)
+        ex = jnp.exp(sc - top)
+        pr = ex * (1.0 / jnp.sum(ex, axis=0, keepdims=True))
+        p_new = jnp.sum(jnp.where(is_new, pr, 0.0), axis=0, keepdims=True).astype(bf16).astype(f32)
+        new_w = jnp.transpose(jnp.broadcast_to(p_new, (HDIM, HDIM)))
+        p_t = jnp.transpose(jnp.where(is_new, 0.0, pr)).astype(bf16)
+        extra = new_w * vs[rows, :]
+        for s in range(NSUB):
+            val_copy(g, s).wait()
+            for j in range(SUB // 4):
+                base = g * GRP + s * SUB + j * 4
+                at = (s * SUB + j * 4) * 4
+                right = jnp.concatenate([vb[base + i] for i in range(4)], axis=1)
+                mix = jnp.dot(p_t[at:at + 16, :], right, preferred_element_type=f32)
+                out = extra[at:at + 16, :]
+                for i in range(4):
+                    out = out + jnp.where(row_i == i, mix[:, i * HDIM:(i + 1) * HDIM], 0.0)
+                cs[pl.ds(pl.multiple_of(g * (GRP * 4) + at, 16), 16), :] = out
+        return carry
+
+    lax.fori_loop(0, NGRP, group, 0)
+
+    ctx = jnp.concatenate([cs[pl.ds(g, ROWS, stride=4), :].astype(bf16) for g in range(heads)], axis=1)
+    load_o.wait()
+    wide = 512
+    for n in range(COLS // wide):
+        part_ref[:, n * wide:(n + 1) * wide] = jnp.dot(
+            ctx, wo[:, n * wide:(n + 1) * wide], preferred_element_type=f32).astype(bf16)
+
+
+def head_call(residual, positions, gain, shift, w_q, w_k, w_v, w_o, keys, vals):
+    bf16 = jnp.bfloat16
+    f32 = jnp.float32
+    vm = pl.BlockSpec(memory_space=pltpu.VMEM)
+    hb = pl.BlockSpec(memory_space=pl.ANY)
+    dma = pltpu.SemaphoreType.DMA
+    nq = w_q.shape[1]
+    return pl.pallas_call(
+        head_kernel,
+        name='head',
+        out_shape=(jax.ShapeDtypeStruct((ROWS, COLS), bf16),
+                   jax.ShapeDtypeStruct((ROWS, HDIM), bf16),
+                   jax.ShapeDtypeStruct((ROWS, HDIM), bf16)),
+        in_specs=[hb, vm, vm, vm, hb, hb, hb, hb, hb, hb],
+        out_specs=(vm, vm, vm),
+        scratch_shapes=[
+            pltpu.VMEM((ROWS, COLS), bf16), pltpu.VMEM((ROWS, COLS), bf16),
+            pltpu.VMEM((COLS, nq + 2 * HDIM), bf16), pltpu.VMEM((nq, COLS), bf16),
+            pltpu.VMEM((ROWS, SEQ, HDIM), bf16), pltpu.VMEM((ROWS, SEQ, HDIM), bf16),
+            pltpu.VMEM((ROWS * 4, HDIM), f32), pltpu.VMEM((ROWS * 4, HDIM), f32),
+            pltpu.VMEM((ROWS * 4, HDIM), f32), pltpu.VMEM((ROWS * 4, HDIM), f32),
+            pltpu.VMEM((ROWS * 4, HDIM), f32),
+            pltpu.VMEM((SEQ, HDIM), f32),
+            dma((2,)), dma((3,)), dma((NGRP, NSUB)), dma((NGRP, NSUB)),
+        ],
+        compiler_params=pltpu.CompilerParams(vmem_limit_bytes=58 * 1024 * 1024),
+    )(residual, positions, gain, shift, w_q, w_k, w_v, w_o, keys, vals)
+
+
 def solution(mesh):
     row_spec = P('dp', None)
     whole_spec = P()
@@ -333,19 +461,10 @@
 
     def local_step(residual, positions, ln1_gain, ln1_shift, w_q, w_k, w_v, w_o, ln2_gain, ln2_shift, w_up, w_down, k_cache, v_cache):
         row_count = residual.shape[0]
-        slots_here = k_cache.shape[2]
-        head_dim = k_cache.shape[3]
-        group_size = w_q.shape[1] // (head_dim * slots_here)
-        normed = layer_norm_1p(residual, ln1_gain, ln1_shift)
-        q_proj = jnp.dot(normed, w_q, preferred_element_type=jnp.float32).astype(jnp.bfloat16)
-        k_proj = jnp.dot(normed, w_k, preferred_element_type=jnp.float32).astype(jnp.bfloat16)
-        v_proj = jnp.dot(normed, w_v, preferred_element_type=jnp.float32).astype(jnp.bfloat16)
-        q_rot = rotate_first_half(q_proj.reshape(row_count, slots_here, group_size, head_dim), positions)
-        k_rot = rotate_first_half(k_proj.reshape(row_count, slots_here, head_dim), positions)
-        v_heads = v_proj.reshape(row_count, slots_here, head_dim)
-        context = attend(q_rot, k_rot, v_heads, k_cache, v_cache, positions)
-        attn_part = jnp.dot(context, w_o, preferred_element_type=jnp.float32).astype(jnp.bfloat16)
+        keys = k_cache.reshape(row_count, k_cache.shape[1], k_cache.shape[3])
+        vals = v_cache.reshape(row_count, v_cache.shape[1], v_cache.shape[3])
+        attn_part, k_rot, v_head = head_call(residual, positions[None, :], ln1_gain[None, :], ln1_shift[None, :], w_q, w_k, w_v, w_o, keys, vals)
         layer_out = tail_call(attn_part, residual, ln2_gain[None, :], ln2_shift[None, :], w_up, w_down)
-        return layer_out, k_rot, v_heads
+        return layer_out, k_rot[:, None, :], v_head[:, None, :]
 
     return jax.shard_map(local_step, mesh=mesh, in_specs=arg_specs, out_specs=(row_spec, new_spec, new_spec), check_vma=False)

time: 83 us -> 87.6 us (1.055)
  Pallas kernels: 45.6 us -> 80.5 us
  matrix products: 23.4 us -> 0 us
  other arithmetic: 6.83 us -> 0 us
    pallas_call x0 -> x1, Pallas kernels: none -> 34.9 us  [head_call(): pl.pallas_call(head_kernel, name='head', out_shape=(jax.ShapeDtypeStruct(...]
    dot_general x6 -> x0, matrix products: 12.1 us -> none  [the longest x1 7.2 us: attend(): jnp.einsum('rkgs,rskd->rkgd', old_probs, v_cache, preferred_element_type=...]
    sub x1 -> x0, matrix products: 11.3 us -> none  [attend(): prob_map = jax.nn.softmax(scores, axis=-1).astype(jnp.bfloat16)]
    reduce_sum x3 -> x0, other arithmetic: 4.92 us -> none  [the longest x1 1.95 us: attend(): jnp.sum(jnp.where(at_pos, prob_map, zero_bf).astype(jnp.float32), axis=-1)]
    broadcast_in_dim x0 -> x2, local copies, waits for them, and re-layouts: none -> 2.59 us  [the longest x1 1.3 us: local_step(): ln1_gain[None, :]]
    unnamed x40 -> x5, local copies, waits for them, and re-layouts: 4.27 us -> 2.01 us
where the time goes in v2:
time: 87.6 us; the launch traced here: 87.1 us
  Pallas kernels  80.5 us (92%)
  local copies, waits for them, and re-layouts  6 us (7%)
    pallas_call x1, Pallas kernels, tail_call(): pl.pallas_call(tail_kernel, name='tail', out_shape=jax.ShapeDtypeStruct((...  45.5 us
    pallas_call x1, Pallas kernels, head_call(): pl.pallas_call(head_kernel, name='head', out_shape=(jax.ShapeDtypeStruct(...  34.9 us
    unnamed x5, local copies, waits for them, and re-layouts  2.01 us

profile of v2, /device:TPU:0, one launch (start us, length us, event | category | flops | bytes accessed | tf_op | source)
XLA Modules:
  0.0 87.1 jit_solution(13313506447946957687)
XLA Ops:
  0.6 1.3 %broadcast_in_dim.22.gain_ref = bf16[1,3072]{1,0:T(2,128)(2,1)} reshape(bf16[3072]{0:T(1024)(128)(2,1)} %param.16) | data formatting | bytes 12288 | tf_op jit(solution)/shard_map/broadcast_in_dim | solution.py:466
  1.9 1.3 %broadcast_in_dim.23.shift_ref = bf16[1,3072]{1,0:T(2,128)(2,1)} reshape(bf16[3072]{0:T(1024)(128)(2,1)} %param.17) | data formatting | bytes 12288 | tf_op jit(solution)/shard_map/broadcast_in_dim | solution.py:466
  3.2 0.7 broadcast_in_dim.24.gain_ref
  3.9 0.7 broadcast_in_dim.25.shift_ref
  4.6 0.0 copy-start
  4.6 34.9 %head.1 = (bf16[128,3072]{1,0:T(8,128)(2,1)}, bf16[128,128]{1,0:T(8,128)(2,1)}, bf16[128,128]{1,0:T(8,128)(2,1)}) custom-call(bf16[128,3072]{1,0:T(8,128)(2,1)} %res_ref.1, s32[1,128]{1,0:T(1,128)} %bitcast.7, bf16[1,3072]{1,0:T(2,128)(2,1)} %broadcast_in_dim.22.gain_ref, bf16[1,3072]{1,0:T(2,128)(2,1)} %broadcast_in_dim.23.shift_ref, ...), custom_call_target="tpu_custom_call" | custom-call | tf_op jit(solution)/shard_map/head/pallas_call | solution.py:431
  39.6 0.0 copy-done
  39.6 0.0 copy-start.1
  39.6 1.1 %copy-done.1 = bf16[128,3072]{1,0:T(8,128)(2,1)S(1)} copy-done((bf16[128,3072]{1,0:T(8,128)(2,1)S(1)}, bf16[128,3072]{1,0:T(8,128)(2,1)}, u32[]{:S(2)}) %copy-start.1) | copy-done | bytes 786456
  40.7 45.5 %tail.1 = bf16[128,3072]{1,0:T(8,128)(2,1)S(1)} custom-call(bf16[128,3072]{1,0:T(8,128)(2,1)S(1)} %copy-done.1, bf16[128,3072]{1,0:T(8,128)(2,1)S(1)} %copy-done, bf16[1,3072]{1,0:T(2,128)(2,1)S(1)} %broadcast_in_dim.24.gain_ref, bf16[1,3072]{1,0:T(2,128)(2,1)S(1)} %broadcast_in_dim.25.shift_ref, bf16[3072,1152]{1,0:T(8,128)(2,1)} %wup_hbm.1, ...), custom_call_target="tpu_custom_call" | custom-call | tf_op jit(solution)/shard_map/tail/pallas_call | solution.py:251
  86.2 0.9 %copy.18 = bf16[128,3072]{1,0:T(8,128)(2,1)} copy(bf16[128,3072]{1,0:T(8,128)(2,1)S(1)} %tail.1) | data formatting | bytes 1572864
Async XLA Ops:
  4.6 34.9 %copy-start = (bf16[128,3072]{1,0:T(8,128)(2,1)S(1)}, bf16[128,3072]{1,0:T(8,128)(2,1)}, u32[]{:S(2)}) copy-start(bf16[128,3072]{1,0:T(8,128)(2,1)} %res_ref.1) | copy-start | bytes 2359300
  39.6 1.1 %copy-start.1 = (bf16[128,3072]{1,0:T(8,128)(2,1)S(1)}, bf16[128,3072]{1,0:T(8,128)(2,1)}, u32[]{:S(2)}) copy-start(bf16[128,3072]{1,0:T(8,128)(2,1)} %get-tuple-element.6.part_ref) | copy-start | bytes 2359300

commit v3 on v2

--- a/solution.py
+++ b/solution.py
@@ -26,7 +26,7 @@
 
 
 def tail_kernel(part_ref, res_ref, gain_ref, shift_ref, wup_hbm, wdn_hbm, out_hbm,
-                wup, wdn, d1, l1, c1, t1, x1, h2, act, p2, d2, l2, c2, t2, obuf,
+                wup, wdn, d1, l1, c1, t1, x1, h2, act, p2, d2, l2, c2, t2, obuf, gs,
                 w_sem, sd1, rd1, sl1, rl1, rc1, shp, rhp, she, rhe,
                 sd2, rd2, sl2, rl2, rc2, sop, rop, soe, roe, o_sem):
     f32 = jnp.float32
@@ -46,6 +46,11 @@
     load_up.start()
     load_dn.start()
 
+    for j in range(COLS // 128):
+        at = slice(j * 128, (j + 1) * 128)
+        gs[0:1, at] = 1.0 + gain_ref[j:j + 1, :].astype(f32)
+        gs[1:2, at] = shift_ref[j:j + 1, :].astype(f32)
+
     barrier = pltpu.get_barrier_semaphore()
     pl.semaphore_signal(barrier, inc=1, device_id={'tp': partner}, device_id_type=MESH_ID)
     pl.semaphore_signal(barrier, inc=1, device_id={'tp': line}, device_id_type=MESH_ID)
@@ -114,7 +119,7 @@
             cent = blk - mean
             var = jnp.mean(cent * cent, axis=-1, keepdims=True)
             nrm = cent * lax.rsqrt(var + LN_EPS)
-            h2[core, m] = (nrm * (1.0 + gain_ref[...].astype(f32)) + shift_ref[...].astype(f32)).astype(bf16)
+            h2[core, m] = (nrm * gs[0:1, :] + gs[1:2, :]).astype(bf16)
             push_h(m).start()
             share_h(m).start()
 
@@ -244,6 +249,7 @@
 
 def tail_call(part, residual, gain, shift, w_up, w_down):
     bf16 = jnp.bfloat16
+    f32 = jnp.float32
     ff = w_up.shape[1]
     vm = pl.BlockSpec(memory_space=pltpu.VMEM)
     hb = pl.BlockSpec(memory_space=pl.ANY)
@@ -264,7 +270,7 @@
             pltpu.VMEM((U2, 2, OWN, CW2), bf16),
             pltpu.VMEM((U2, OWN, CW2), bf16), pltpu.VMEM((U2, OWN, CW2), bf16),
             pltpu.VMEM((U2, OWN, CW2), bf16), pltpu.VMEM((U2, OWN, CW2), bf16),
-            pltpu.VMEM((U2, 2, OWN, CW2), bf16),
+            pltpu.VMEM((U2, 2, OWN, CW2), bf16), pltpu.VMEM((2, COLS), f32),
             dma((2,)),
             dma((U1,)), dma((U1,)), dma((U1,)), dma((U1,)), dma((U1,)),
             dma((MSG,)), dma((MSG,)), dma((MSG,)), dma((MSG,)),
@@ -280,47 +286,50 @@
 SEQ = 512
 GRP = 32
 NGRP = ROWS // GRP
-SUB = 8
-NSUB = GRP // SUB
+TCH = 128
 ROT = 64
 
 
 def head_kernel(x_hbm, pos_ref, gain_ref, shift_ref, wq_hbm, wk_hbm, wv_hbm, wo_hbm, k_hbm, v_hbm,
                 part_ref, knew_ref, vnew_ref,
-                xs, hs, wqkv, wo, kb, vb, qs, ks, vs, ps, cs, ss,
+                xs, hs, wq, wk, wv, wo, kb, vb, qs, ks, vs, ps, cs, qb, gs, ord_v, ord_s, perm, perm_t,
                 in_sem, w_sem, k_sem, v_sem):
     f32 = jnp.float32
     bf16 = jnp.bfloat16
-    nq = wq_hbm.shape[1]
+    heads = wq_hbm.shape[1] // HDIM
 
     load_x = pltpu.make_async_copy(x_hbm, xs, in_sem.at[0])
-    load_q = pltpu.make_async_copy(wq_hbm, wqkv.at[:, pl.ds(0, nq)], w_sem.at[0])
-    load_k = pltpu.make_async_copy(wk_hbm, wqkv.at[:, pl.ds(nq, HDIM)], w_sem.at[1])
-    load_v = pltpu.make_async_copy(wv_hbm, wqkv.at[:, pl.ds(nq + HDIM, HDIM)], w_sem.at[2])
+    load_q = pltpu.make_async_copy(wq_hbm, wq, w_sem.at[0])
+    load_k = pltpu.make_async_copy(wk_hbm, wk, w_sem.at[1])
+    load_v = pltpu.make_async_copy(wv_hbm, wv, w_sem.at[2])
     load_o = pltpu.make_async_copy(wo_hbm, wo, in_sem.at[1])
-
-    def key_copy(g, s):
-        at = pl.ds(g * GRP + s * SUB, SUB)
-        return pltpu.make_async_copy(k_hbm.at[at], kb.at[at], k_sem.at[g, s])
-
-    def val_copy(g, s):
-        at = pl.ds(g * GRP + s * SUB, SUB)
-        return pltpu.make_async_copy(v_hbm.at[at], vb.at[at], v_sem.at[g, s])
-
+    move_ord = pltpu.make_async_copy(ord_v, ord_s, in_sem.at[2])
     load_x.start()
     load_q.start()
     load_k.start()
     load_v.start()
-    for g in range(NGRP):
-        for s in range(NSUB):
-            key_copy(g, s).start()
-        if g == NGRP - 1:
-            load_o.start()
-        for s in range(NSUB):
-            val_copy(g, s).start()
 
     lane = lax.broadcasted_iota(jnp.int32, (ROWS, HDIM), 1)
-    pos_col = jnp.transpose(jnp.broadcast_to(pos_ref[...].astype(f32), (ROWS, ROWS)))
+    sub = lax.broadcasted_iota(jnp.int32, (ROWS, HDIM), 0)
+    pos_lane = jnp.broadcast_to(pos_ref[...].astype(f32), (ROWS, ROWS))
+    pos_col = jnp.transpose(pos_lane)
+    ahead = jnp.logical_or(pos_col > pos_lane, jnp.logical_and(pos_col == pos_lane, sub < lane))
+    rank = jnp.sum(jnp.where(ahead, 1.0, 0.0), axis=0, keepdims=True)
+    hot = jnp.where(sub.astype(f32) == rank, 1.0, 0.0)
+    hot_t = jnp.transpose(hot)
+    perm[...] = hot.astype(bf16)
+    perm_t[...] = hot_t.astype(bf16)
+    order = jnp.sum(hot_t * sub.astype(f32), axis=0, keepdims=True)
+    spos = jnp.sum(hot_t * pos_col, axis=0, keepdims=True)
+    ord_v[0:1, :] = order.astype(jnp.int32)
+    ord_v[1:2, :] = spos.astype(jnp.int32)
+
+    for j in range(COLS // HDIM):
+        at = slice(j * HDIM, (j + 1) * HDIM)
+        gs[0:1, at] = 1.0 + gain_ref[j:j + 1, :].astype(f32)
+        gs[1:2, at] = shift_ref[j:j + 1, :].astype(f32)
+    move_ord.start()
+
     half = ROT // 2
     pair = lax.rem(lane, half).astype(f32)
     inv = jnp.exp(pair * (-2.0 * math.log(ROPE_BASE) / ROT))
@@ -334,62 +343,80 @@
         swap = jnp.where(lane < half, pltpu.roll(v, HDIM - half, 1), pltpu.roll(v, half, 1))
         return (v * cos_t + swap * sin_t).astype(bf16)
 
+    def chunks(g):
+        return lax.div(ord_s[1, g * GRP], TCH) + 1
+
+    move_ord.wait()
+    for g in range(NGRP):
+        size = pl.multiple_of(chunks(g) * TCH, TCH)
+
+        def fetch(hbm, buf, sem):
+            def one(i, carry):
+                slot = g * GRP + i
+                src = pl.ds(pl.multiple_of(ord_s[0, slot] * SEQ, SEQ), size)
+                dst = pl.ds(pl.multiple_of(slot * SEQ, SEQ), size)
+                pltpu.make_async_copy(hbm.at[src], buf.at[dst], sem.at[g]).start()
+                return carry
+            lax.fori_loop(0, GRP, one, 0, unroll=8)
+
+        fetch(k_hbm, kb, k_sem)
+        fetch(v_hbm, vb, v_sem)
+    load_o.start()
+
     load_x.wait()
-    rb = 32
-    gain1 = 1.0 + gain_ref[...].astype(f32)
-    shift1 = shift_ref[...].astype(f32)
+    rb = 16
     for r in range(ROWS // rb):
         blk = xs[r * rb:(r + 1) * rb, :].astype(f32)
         mean = jnp.mean(blk, axis=-1, keepdims=True)
         cent = blk - mean
         var = jnp.mean(cent * cent, axis=-1, keepdims=True)
         nrm = cent * lax.rsqrt(var + LN_EPS)
-        hs[r * rb:(r + 1) * rb, :] = (nrm * gain1 + shift1).astype(bf16)
+        hs[r * rb:(r + 1) * rb, :] = (nrm * gs[0:1, :] + gs[1:2, :]).astype(bf16)
 
     load_q.wait()
     load_k.wait()
     load_v.wait()
-    qkv = jnp.dot(hs[...], wqkv[...], preferred_element_type=f32).astype(bf16).astype(f32)
-    k_rot = rotate(qkv[:, nq:nq + HDIM])
-    v_head = qkv[:, nq + HDIM:nq + 2 * HDIM]
+    qp = jnp.dot(hs[...], wq[...], preferred_element_type=f32).astype(bf16).astype(f32)
+    kp = jnp.dot(hs[...], wk[...], preferred_element_type=f32).astype(bf16).astype(f32)
+    vp = jnp.dot(hs[...], wv[...], preferred_element_type=f32).astype(bf16)
+    k_rot = rotate(kp)
     knew_ref[...] = k_rot
-    vnew_ref[...] = v_head.astype(bf16)
-    heads = nq // HDIM
+    vnew_ref[...] = vp
     for g in range(4):
         at = pl.ds(g, ROWS, stride=4)
         if g < heads:
-            qs[at, :] = rotate(qkv[:, g * HDIM:(g + 1) * HDIM]).astype(f32)
+            turned = rotate(qp[:, g * HDIM:(g + 1) * HDIM])
+            qs[at, :] = jnp.dot(perm[...], turned, preferred_element_type=f32)
         else:
             qs[at, :] = jnp.zeros((ROWS, HDIM), f32)
-        ks[at, :] = k_rot.astype(f32)
-        vs[at, :] = v_head
-        ps[at, :] = pos_col
+    k_sort = jnp.dot(perm[...], k_rot, preferred_element_type=f32)
+    v_sort = jnp.dot(perm[...], vp, preferred_element_type=f32)
+    p_sort = jnp.transpose(jnp.broadcast_to(ord_v[1:2, :].astype(f32), (ROWS, ROWS)))
+    for g in range(4):
+        at = pl.ds(g, ROWS, stride=4)
+        ks[at, :] = k_sort
+        vs[at, :] = v_sort
+        ps[at, :] = p_sort
 
     scale = 1.0 / math.sqrt(HDIM)
     lane_b = lax.div(lane, 4)
     row_i = lax.div(lax.broadcasted_iota(jnp.int32, (16, HDIM), 0), 4)
-    step_t = lax.broadcasted_iota(jnp.int32, (SEQ, HDIM), 0)
-
-    def group(g, carry):
-        rows = pl.ds(pl.multiple_of(g * (GRP * 4), GRP * 4), GRP * 4)
-        qg = qs[rows, :]
-        q_t = jnp.transpose(qg)
-        p_row = jnp.transpose(ps[rows, :])[0:1, :].astype(jnp.int32)
-        new_col = jnp.sum(qg * ks[rows, :], axis=-1, keepdims=True)
-        new_row = jnp.transpose(jnp.broadcast_to(new_col, (HDIM, HDIM)))[0:1, :]
-        for s in range(NSUB):
-            key_copy(g, s).wait()
-            base = g * GRP + s * SUB
-            left = jnp.concatenate([kb[base + i] for i in range(SUB)], axis=1)
-            right = jnp.concatenate(
-                [jnp.where(lane_b == s * SUB + i, q_t, 0.0).astype(bf16) for i in range(SUB)], axis=0)
-            acc = jnp.dot(left, right, preferred_element_type=f32)
-            if s == 0:
-                ss[...] = acc
-            else:
-                ss[...] += acc
+
+    def attend(g, rows, p_row, new_row, span):
+        size = GRP * span
+        at_all = pl.ds(0, size)
+        pltpu.make_async_copy(k_hbm.at[at_all], kb.at[at_all], k_sem.at[g]).wait()
+
+        def tile(buf, i, lo, n):
+            return buf[pl.ds(pl.multiple_of((g * GRP + i) * SEQ, SEQ) + lo, n), :]
+
+        part = span // 2
+        raw = [jnp.dot(
+            jnp.concatenate([tile(kb, i, h * part, part) for i in range(GRP)], axis=1),
+            qb[...], preferred_element_type=f32) for h in range(2)]
+        step_t = lax.broadcasted_iota(jnp.int32, (span, HDIM), 0)
         is_new = step_t == p_row
-        sc = jnp.where(is_new, new_row, ss[...]) * scale
+        sc = jnp.where(is_new, new_row, jnp.concatenate(raw, axis=0)) * scale
         sc = jnp.where(step_t <= p_row, sc, -jnp.inf)
         top = jnp.max(sc, axis=0, keepdims=True)
         ex = jnp.exp(sc - top)
@@ -398,22 +425,36 @@
         new_w = jnp.transpose(jnp.broadcast_to(p_new, (HDIM, HDIM)))
         p_t = jnp.transpose(jnp.where(is_new, 0.0, pr)).astype(bf16)
         extra = new_w * vs[rows, :]
-        for s in range(NSUB):
-            val_copy(g, s).wait()
-            for j in range(SUB // 4):
-                base = g * GRP + s * SUB + j * 4
-                at = (s * SUB + j * 4) * 4
-                right = jnp.concatenate([vb[base + i] for i in range(4)], axis=1)
-                mix = jnp.dot(p_t[at:at + 16, :], right, preferred_element_type=f32)
-                out = extra[at:at + 16, :]
-                for i in range(4):
-                    out = out + jnp.where(row_i == i, mix[:, i * HDIM:(i + 1) * HDIM], 0.0)
-                cs[pl.ds(pl.multiple_of(g * (GRP * 4) + at, 16), 16), :] = out
+        pltpu.make_async_copy(v_hbm.at[at_all], vb.at[at_all], v_sem.at[g]).wait()
+        for j in range(GRP // 4):
+            at = j * 16
+            right = jnp.concatenate([tile(vb, j * 4 + i, 0, span) for i in range(4)], axis=1)
+            mix = jnp.dot(p_t[at:at + 16, :], right, preferred_element_type=f32)
+            out = extra[at:at + 16, :]
+            for i in range(4):
+                out = out + jnp.where(row_i == i, mix[:, i * HDIM:(i + 1) * HDIM], 0.0)
+            cs[pl.ds(pl.multiple_of(g * (GRP * 4) + at, 16), 16), :] = out
+
+    def group(g, carry):
+        rows = pl.ds(pl.multiple_of(g * (GRP * 4), GRP * 4), GRP * 4)
+        qg = qs[rows, :]
+        q_t = jnp.transpose(qg)
+        p_row = jnp.transpose(ps[rows, :])[0:1, :].astype(jnp.int32)
+        new_col = jnp.sum(qg * ks[rows, :], axis=-1, keepdims=True)
+        new_row = jnp.transpose(jnp.broadcast_to(new_col, (HDIM, HDIM)))[0:1, :]
+        for i in range(GRP):
+            qb[i * HDIM:(i + 1) * HDIM, :] = jnp.where(lane_b == i, q_t, 0.0).astype(bf16)
+        count = chunks(g)
+        for n in range(1, SEQ // TCH + 1):
+            @pl.when(count == n)
+            def _():
+                attend(g, rows, p_row, new_row, n * TCH)
         return carry
 
     lax.fori_loop(0, NGRP, group, 0)
 
     ctx = jnp.concatenate([cs[pl.ds(g, ROWS, stride=4), :].astype(bf16) for g in range(heads)], axis=1)
+    ctx = jnp.dot(perm_t[...], ctx, preferred_element_type=f32).astype(bf16)
     load_o.wait()
     wide = 512
     for n in range(COLS // wide):
@@ -438,13 +479,16 @@
         out_specs=(vm, vm, vm),
         scratch_shapes=[
             pltpu.VMEM((ROWS, COLS), bf16), pltpu.VMEM((ROWS, COLS), bf16),
-            pltpu.VMEM((COLS, nq + 2 * HDIM), bf16), pltpu.VMEM((nq, COLS), bf16),
-            pltpu.VMEM((ROWS, SEQ, HDIM), bf16), pltpu.VMEM((ROWS, SEQ, HDIM), bf16),
+            pltpu.VMEM((COLS, nq), bf16), pltpu.VMEM((COLS, HDIM), bf16), pltpu.VMEM((COLS, HDIM), bf16),
+            pltpu.VMEM((nq, COLS), bf16),
+            pltpu.VMEM((ROWS * SEQ, HDIM), bf16), pltpu.VMEM((ROWS * SEQ, HDIM), bf16),
             pltpu.VMEM((ROWS * 4, HDIM), f32), pltpu.VMEM((ROWS * 4, HDIM), f32),
             pltpu.VMEM((ROWS * 4, HDIM), f32), pltpu.VMEM((ROWS * 4, HDIM), f32),
             pltpu.VMEM((ROWS * 4, HDIM), f32),
-            pltpu.VMEM((SEQ, HDIM), f32),
-            dma((2,)), dma((3,)), dma((NGRP, NSUB)), dma((NGRP, NSUB)),
+            pltpu.VMEM((GRP * HDIM, HDIM), bf16), pltpu.VMEM((2, COLS), f32),
+            pltpu.VMEM((8, ROWS), jnp.int32), pltpu.SMEM((8, ROWS), jnp.int32),
+            pltpu.VMEM((ROWS, ROWS), bf16), pltpu.VMEM((ROWS, ROWS), bf16),
+            dma((3,)), dma((3,)), dma((NGRP,)), dma((NGRP,)),
         ],
         compiler_params=pltpu.CompilerParams(vmem_limit_bytes=58 * 1024 * 1024),
     )(residual, positions, gain, shift, w_q, w_k, w_v, w_o, keys, vals)
@@ -461,10 +505,10 @@
 
     def local_step(residual, positions, ln1_gain, ln1_shift, w_q, w_k, w_v, w_o, ln2_gain, ln2_shift, w_up, w_down, k_cache, v_cache):
         row_count = residual.shape[0]
-        keys = k_cache.reshape(row_count, k_cache.shape[1], k_cache.shape[3])
-        vals = v_cache.reshape(row_count, v_cache.shape[1], v_cache.shape[3])
-        attn_part, k_rot, v_head = head_call(residual, positions[None, :], ln1_gain[None, :], ln1_shift[None, :], w_q, w_k, w_v, w_o, keys, vals)
-        layer_out = tail_call(attn_part, residual, ln2_gain[None, :], ln2_shift[None, :], w_up, w_down)
+        keys = k_cache.reshape(row_count * k_cache.shape[1], k_cache.shape[3])
+        vals = v_cache.reshape(row_count * v_cache.shape[1], v_cache.shape[3])
+        attn_part, k_rot, v_head = head_call(residual, positions[None, :], ln1_gain.reshape(COLS // 128, 128), ln1_shift.reshape(COLS // 128, 128), w_q, w_k, w_v, w_o, keys, vals)
+        layer_out = tail_call(attn_part, residual, ln2_gain.reshape(COLS // 128, 128), ln2_shift.reshape(COLS // 128, 128), w_up, w_down)
         return layer_out, k_rot[:, None, :], v_head[:, None, :]
 
     return jax.shard_map(local_step, mesh=mesh, in_specs=arg_specs, out_specs=(row_spec, new_spec, new_spec), check_vma=False)

time: 87.6 us -> 63.4 us (0.72)
  Pallas kernels: 80.5 us -> 60.7 us
  local copies, waits for them, and re-layouts: 6 us -> 2.02 us
    pallas_call x1, Pallas kernels: 34.9 us -> 15 us  [head_call(): pl.pallas_call(head_kernel, name='head', out_shape=(jax.ShapeDtypeStruct(...]
    broadcast_in_dim x4 -> x0, local copies, waits for them, and re-layouts: 3.99 us -> none  [the longest x1 1.3 us: local_step(): ln1_gain[None, :]]
    unnamed x5 -> x9, local copies, waits for them, and re-layouts: 2.01 us -> 2.02 us
where the time goes in v3:
time: 63.4 us
  Pallas kernels  60.7 us (96%)
  local copies, waits for them, and re-layouts  2.02 us (3%)
  between operations  0.71 us (1%)
    pallas_call x1, Pallas kernels, tail_call(): pl.pallas_call(tail_kernel, name='tail', out_shape=jax.ShapeDtypeStruct((...  45.7 us
    pallas_call x1, Pallas kernels, head_call(): pl.pallas_call(head_kernel, name='head', out_shape=(jax.ShapeDtypeStruct(...  15 us
    unnamed x9, local copies, waits for them, and re-layouts  2.02 us

profile of v3, /device:TPU:0, one launch (start us, length us, event | category | flops | bytes accessed | tf_op | source)
XLA Modules:
  0.0 63.4 jit_solution(7416033573927375379)
XLA Ops:
  0.6 0.0 copy-start
  0.6 0.0 copy-start.2
  0.7 0.0 copy-start.3
  0.7 15.0 %head.1 = (bf16[128,3072]{1,0:T(8,128)(2,1)}, bf16[128,128]{1,0:T(8,128)(2,1)}, bf16[128,128]{1,0:T(8,128)(2,1)}) custom-call(bf16[128,3072]{1,0:T(8,128)(2,1)} %res_ref.1, s32[1,128]{1,0:T(1,128)} %bitcast.15, bf16[24,128]{1,0:T(8,128)(2,1)} %bitcast.13, bf16[24,128]{1,0:T(8,128)(2,1)} %bitcast.14, bf16[3072,384]{1,0:T(8,128)(2,1)} %wq_hbm.1, ...), custom_call_target="tpu_custom_call" | custom-call | tf_op jit(solution)/shard_map/head/pallas_call | solution.py:472
  15.7 0.0 copy-done
  15.7 0.0 copy-done.2
  15.7 0.0 copy-done.3
  15.7 0.0 copy-start.1
  15.7 1.1 %copy-done.1 = bf16[128,3072]{1,0:T(8,128)(2,1)S(1)} copy-done((bf16[128,3072]{1,0:T(8,128)(2,1)S(1)}, bf16[128,3072]{1,0:T(8,128)(2,1)}, u32[]{:S(2)}) %copy-start.1) | copy-done | bytes 786456
  16.8 45.7 %tail.1 = bf16[128,3072]{1,0:T(8,128)(2,1)S(1)} custom-call(bf16[128,3072]{1,0:T(8,128)(2,1)S(1)} %copy-done.1, bf16[128,3072]{1,0:T(8,128)(2,1)S(1)} %copy-done, bf16[24,128]{1,0:T(8,128)(2,1)S(1)} %bitcast.9, bf16[24,128]{1,0:T(8,128)(2,1)S(1)} %bitcast.10, bf16[3072,1152]{1,0:T(8,128)(2,1)} %wup_hbm.1, bf16[1152,3072]{1,0:T(8,128)(2,1)} %wdn_hbm.1), custom_call_target="tpu_custom_call" | custom-call | tf_op jit(solution)/shard_map/tail/pallas_call | solution.py:257
  62.6 0.9 %copy.18 = bf16[128,3072]{1,0:T(8,128)(2,1)} copy(bf16[128,3072]{1,0:T(8,128)(2,1)S(1)} %tail.1) | data formatting | bytes 1572864
Async XLA Ops:
  0.6 15.0 %copy-start = (bf16[128,3072]{1,0:T(8,128)(2,1)S(1)}, bf16[128,3072]{1,0:T(8,128)(2,1)}, u32[]{:S(2)}) copy-start(bf16[128,3072]{1,0:T(8,128)(2,1)} %res_ref.1) | copy-start | bytes 2359300
  0.6 15.0 %copy-start.2 = (bf16[3072]{0:T(1024)(128)(2,1)S(1)}, bf16[3072]{0:T(1024)(128)(2,1)}, u32[]{:S(2)}) copy-start(bf16[3072]{0:T(1024)(128)(2,1)} %param.22) | copy-start | bytes 18436
  0.7 15.0 %copy-start.3 = (bf16[3072]{0:T(1024)(128)(2,1)S(1)}, bf16[3072]{0:T(1024)(128)(2,1)}, u32[]{:S(2)}) copy-start(bf16[3072]{0:T(1024)(128)(2,1)} %param.23) | copy-start | bytes 18436
  15.7 1.1 %copy-start.1 = (bf16[128,3072]{1,0:T(8,128)(2,1)S(1)}, bf16[128,3072]{1,0:T(8,128)(2,1)}, u32[]{:S(2)}) copy-start(bf16[128,3072]{1,0:T(8,128)(2,1)} %get-tuple-element.6.part_ref) | copy-start | bytes 2359300
